TPU v7x, 32 devices: a whole 2x2x4 slice. The times are simulated.
32 devices in a mesh: units: 8 (over z, x), expert: 4 (over y, core).
Axes of the slice: x: 2, y: 2, z: 4, core: 2. Of those that a mesh axis runs over, the one named last changes fastest.
Arguments:
- a_up: float32 [57344, 2048], P(('expert', 'units')), parts along dimension 0, may hold values from -6 to 6
- a_down: float32 [57344, 2048], P(('expert', 'units')), parts along dimension 0, may hold values from -6 to 6
- b_up: float32 [57344, 2048], P(('expert', 'units')), parts along dimension 0, may hold values from -6 to 6
- b_down: float32 [57344, 2048], P(('expert', 'units')), parts along dimension 0, may hold values from -6 to 6
- perm: int32 [57344], P('expert'), parts along dimension 0, may hold values from 0 to 14335, as said below
Outputs:
- merged_up: float32 [57344, 2048], P(('expert', 'units')), parts along dimension 0
- merged_down: float32 [57344, 2048], P(('expert', 'units')), parts along dimension 0
There are 4 independent parts, one for each index of `expert`. A program takes and returns all parts, laid end to end along the dimension named above; each array names one. Nothing has to cross between parts.
Inputs may be any that keep to these rules, and one draw needn't show every extreme that they name: perm names each of the 14336 units once. Cut the units into aligned blocks of 1792: of the units of one source block, at most 225 are matched to units of any one destination block, and in every draw some pair of blocks reaches 225. Every source block sends the same list of counts to the destination blocks, in an order that differs from source to source.
All inputs are finite; a program needn't handle non-finite values.
Results may differ from a plain program's by a relative error of at most 0.00002.
Values sent between devices are 32-bit elements; how exact they have to be, the bound alone decides.
A program may use at most 192 MiB of HBM per device.

v0:
```python
import math

import jax
import jax.numpy as jnp
from jax import lax
from jax.sharding import PartitionSpec as P


def on_device(a_up, a_down, b_up, b_down, perm):
    count = lax.axis_size("units")
    me_index = lax.axis_index("units")
    rows = b_up.shape[0]
    limit = (rows + count - 1) // count + 1
    total = perm.shape[0]
    mine = me_index * rows + jnp.arange(rows, dtype=jnp.int32)
    turns = math.gcd(count, 8)
    block = total // turns
    own_targets = jnp.zeros((rows,), jnp.int32)
    for turn in range(turns):
        segment = perm[turn * block : (turn + 1) * block]
        owners = (turn * block + jnp.arange(block, dtype=jnp.int32)) // rows
        hits = (segment[None, :] == mine[:, None]).astype(jnp.int32)
        own_targets = own_targets + jnp.sum(hits * owners[None, :], axis=1)
    position = jnp.arange(rows, dtype=jnp.int32)
    same_target = (own_targets[None, :] == own_targets[:, None]).astype(jnp.int32)
    before_me = (position[None, :] < position[:, None]).astype(jnp.int32)
    ranking = jnp.sum(same_target * before_me, axis=1)
    keyed = own_targets * limit + ranking
    slot_ids = jnp.arange(count * limit, dtype=jnp.int32)
    matches = (keyed[None, :] == slot_ids[:, None]).astype(jnp.int32)
    slots = jnp.sum(matches * position[None, :], axis=1) + rows * (1 - jnp.sum(matches, axis=1))
    own_sources = lax.dynamic_slice_in_dim(perm, me_index * rows, rows)
    source_dev = own_sources // rows
    same_source = (source_dev[None, :] == source_dev[:, None]).astype(jnp.int32)
    smaller = (own_sources[None, :] < own_sources[:, None]).astype(jnp.int32)
    picks = source_dev * limit + jnp.sum(same_source * smaller, axis=1)

    def pack(matrix):
        return jnp.take(matrix, slots, axis=0, mode="fill", fill_value=0.0)

    def unpack(received, own):
        return (own + jnp.take(received, picks, axis=0)) * 0.5

    got_up, got_down = (
        lax.all_to_all(pack(b_up), "units", split_axis=0, concat_axis=0, tiled=True),
        lax.all_to_all(pack(b_down), "units", split_axis=0, concat_axis=0, tiled=True),
    )
    merged_up = unpack(got_up, a_up)
    merged_down = unpack(got_down, a_down)
    return (merged_up, merged_down)


def solution(mesh):
    return jax.shard_map(
        on_device,
        mesh=mesh,
        in_specs=(
            P(("expert", "units"), None),
            P(("expert", "units"), None),
            P(("expert", "units"), None),
            P(("expert", "units"), None),
            P("expert"),
        ),
        out_specs=(P(("expert", "units"), None), P(("expert", "units"), None)),
        check_vma=False,
    )
```

profile of v0, /device:TPU:0, one launch (start us, length us, event | category | flops | bytes accessed | tf_op | source)
XLA Modules:
  0.0 823.6 jit_solution(16662388927000129957)
XLA Ops:
  0.7 0.9 add_select_fusion
  1.6 11.2 %select_reduce_fusion.9 = (s32[1792]{0:T(1024)S(1)}, s32[1792]{0:T(1024)S(1)}, s32[1792]{0:T(1024)S(1)}, s32[1792]{0:T(1024)S(1)}, s32[1792]{0:T(1024)S(1)}, /*i...) fusion(s32[1792]{0:T(1024)S(1)} %get-tuple-element.38, s32[1792]{0:T(1024)S(1)} %get-tuple-element.25, ...), kind=kLoop, calls=%fused_computation.20 | loop fusion | flops 77056000 | bytes 179200 | tf_op jit(solution)/shard_map/reduce_sum | solution.py:23
  12.8 0.9 select_reduce_fusion.2
  13.8 3.9 convert_reduce_fusion
  17.7 20.6 %gather_fusion.2 = f32[1800,2048]{1,0:T(8,128)} fusion(f32[1792,2048]{1,0:T(8,128)} %param.12, s32[2048]{0:T(1024)S(1)} %pad_clamp_fusion.1), kind=kCustom, calls=%fused_computation.2.clone | custom fusion | bytes 29498400 | tf_op jit(solution)/shard_map/jit(_take)/gather | solution.py:39
  38.3 20.6 %gather_fusion = f32[1800,2048]{1,0:T(8,128)} fusion(f32[1792,2048]{1,0:T(8,128)} %param.11, s32[2048]{0:T(1024)S(1)} %pad_clamp_fusion.1), kind=kCustom, calls=%fused_computation.clone | custom fusion | bytes 29498400 | tf_op jit(solution)/shard_map/jit(_take)/gather | solution.py:39
  58.9 20.4 %broadcast_select_fusion = (f32[1800,2048]{1,0:T(8,128)}, f32[1800,2048]{1,0:T(8,128)}) fusion(f32[1800,2048]{1,0:T(8,128)} %gather_fusion.2, pred[1800]{0:T(1024)(128)(4,1)S(1)} %get-tuple-element.18, f32[1800,2048]{1,0:T(8,128)} %gather_fusion), kind=kLoop, calls=%fused_computation.22 | loop fusion | flops 7372800 | bytes 58984200 | tf_op jit(solution)/shard_map/jit(_take)/select_n | solution.py:39
  79.3 12.3 %all_to_all.19 = f32[8,225,2048]{2,1,0:T(8,128)} reshape(f32[1800,2048]{1,0:T(8,128)} %get-tuple-element.30) | data formatting | bytes 29491200 | tf_op jit(solution)/shard_map/all_to_all | solution.py:46
  91.7 7.3 all-to-all-start.1
  99.0 12.3 %all_to_all.16 = f32[8,225,2048]{2,1,0:T(8,128)} reshape(f32[1800,2048]{1,0:T(8,128)} %get-tuple-element.31) | data formatting | bytes 29491200 | tf_op jit(solution)/shard_map/all_to_all | solution.py:45
  111.3 316.9 %all-to-all-done.1 = f32[8,225,2048]{2,1,0:T(8,128)} async-done(((f32[8,225,2048]{2,1,0:T(8,128)}), f32[8,225,2048]{2,1,0:T(8,128)}, u32[]{:S(2)}, u32[]{:S(2)}) %all-to-all-start.1) | async-done | bytes 14745632 | tf_op jit(solution)/shard_map/all_to_all | solution.py:46
  428.2 5.6 all-to-all-start
  433.8 2.6 select_reduce_fusion.1
  436.4 12.3 %all_to_all.21 = f32[1800,2048]{1,0:T(8,128)} reshape(f32[8,225,2048]{2,1,0:T(8,128)} %all-to-all-done.1) | data formatting | bytes 29491200 | tf_op jit(solution)/shard_map/all_to_all | solution.py:46
  448.7 19.5 %gather_fusion.3 = f32[1792,2048]{1,0:T(8,128)} fusion(f32[1800,2048]{1,0:T(8,128)} %all_to_all.21, s32[2048]{0:T(1024)S(1)} %pad_clamp_fusion), kind=kCustom, calls=%fused_computation.3.clone | custom fusion | bytes 29367296 | tf_op jit(solution)/shard_map/jit(_take)/gather | solution.py:42
  468.2 293.8 %all-to-all-done = f32[8,225,2048]{2,1,0:T(8,128)} async-done(((f32[8,225,2048]{2,1,0:T(8,128)}), f32[8,225,2048]{2,1,0:T(8,128)}, u32[]{:S(2)}, u32[]{:S(2)}) %all-to-all-start) | async-done | bytes 14745632 | tf_op jit(solution)/shard_map/all_to_all | solution.py:45
  762.1 12.3 %all_to_all.18 = f32[1800,2048]{1,0:T(8,128)} reshape(f32[8,225,2048]{2,1,0:T(8,128)} %all-to-all-done) | data formatting | bytes 29491200 | tf_op jit(solution)/shard_map/all_to_all | solution.py:45
  774.4 19.5 %gather_fusion.1 = f32[1792,2048]{1,0:T(8,128)} fusion(f32[1800,2048]{1,0:T(8,128)} %all_to_all.18, s32[2048]{0:T(1024)S(1)} %pad_clamp_fusion), kind=kCustom, calls=%fused_computation.1.clone | custom fusion | bytes 29367296 | tf_op jit(solution)/shard_map/jit(_take)/gather | solution.py:42
  793.9 29.7 %fusion = (f32[1792,2048]{1,0:T(8,128)}, f32[1792,2048]{1,0:T(8,128)}) fusion(f32[1792,2048]{1,0:T(8,128)} %param.10, f32[1792,2048]{1,0:T(8,128)} %gather_fusion.3, pred[1792]{0:T(1024)(128)(4,1)S(1)} %get-tuple-element.14, f32[1792,2048]{1,0:T(8,128)} %param.9, f32[1792,2048]{1,0:T(8,128)} %gather_fusion.1), kind=kLoop, calls=%fused_computation.5 | loop fusion | flops 22020096 | bytes 88082176 | tf_op jit(solution)/shard_map/mul | solution.py:42
  (10 shorter events, 0.1 us)
Async XLA Ops:
  91.7 336.5 %all-to-all-start.1 = ((f32[8,225,2048]{2,1,0:T(8,128)}), f32[8,225,2048]{2,1,0:T(8,128)}, u32[]{:S(2)}, u32[]{:S(2)}) async-start(f32[8,225,2048]{2,1,0:T(8,128)} %all_to_all.19), calls=%async_computation.1 | async-start | bytes 30408704 | tf_op jit(solution)/shard_map/all_to_all | solution.py:46
  428.2 333.9 %all-to-all-start = ((f32[8,225,2048]{2,1,0:T(8,128)}), f32[8,225,2048]{2,1,0:T(8,128)}, u32[]{:S(2)}, u32[]{:S(2)}) async-start(f32[8,225,2048]{2,1,0:T(8,128)} %all_to_all.16), calls=%async_computation | async-start | bytes 30408704 | tf_op jit(solution)/shard_map/all_to_all | solution.py:45
where the time goes:
time: 824 us
  waiting for transfers between devices  611 us (74%)
  local copies, waits for them, and re-layouts  129 us (16%)
  other arithmetic  69.8 us (8%)
  starting transfers between devices  12.9 us (2%)
    all_to_all x1, waiting for transfers between devices, on_device(): lax.all_to_all(pack(b_down), 'units', split_axis=0, concat_axis=0, tiled=...  317 us
    all_to_all x1, waiting for transfers between devices, on_device(): lax.all_to_all(pack(b_up), 'units', split_axis=0, concat_axis=0, tiled=True)  294 us
    gather x2, local copies, waits for them, and re-layouts, pack(): return jnp.take(matrix, slots, axis=0, mode='fill', fill_value=0.0)  41.2 us
    gather x2, local copies, waits for them, and re-layouts, unpack(): return (own + jnp.take(received, picks, axis=0)) * 0.5  39 us
    mul x1, other arithmetic, unpack(): return (own + jnp.take(received, picks, axis=0)) * 0.5  29.7 us
    all_to_all x2, local copies, waits for them, and re-layouts, on_device(): lax.all_to_all(pack(b_down), 'units', split_axis=0, concat_axis=0, tiled=...  24.7 us
    all_to_all x2, local copies, waits for them, and re-layouts, on_device(): lax.all_to_all(pack(b_up), 'units', split_axis=0, concat_axis=0, tiled=True)  24.7 us
    select_n x1, other arithmetic, pack(): return jnp.take(matrix, slots, axis=0, mode='fill', fill_value=0.0)  20.4 us
  transfers between devices with their start and end apart: 2, of which 2 were waited for; matrix products, arithmetic and copies ran while one was open for 3% of the time, Pallas kernels for 0%

commit v1 on v0

v1 whole, which is shorter than its diff:
```python
import functools

import jax
import jax.numpy as jnp
from jax import lax
from jax.experimental import pallas as pl
from jax.experimental.pallas import tpu as pltpu
from jax.sharding import PartitionSpec as P

LANES = 256
UNROLL = 25


def index_lists(perm, rows, count, limit, me):
    base = me * rows
    table = perm.reshape(count, rows)
    mine = (table >= base) & (table < base + rows)
    upto = jnp.arange(rows, dtype=jnp.int32)
    earlier = (upto[:, None] < upto[None, :]).astype(jnp.bfloat16)
    rank = jnp.dot(mine.astype(jnp.bfloat16), earlier, preferred_element_type=jnp.float32).astype(jnp.int32)
    rank = jnp.where(mine, rank, -1)
    local = jnp.where(mine, table - base, 0)
    ids = jnp.arange(limit, dtype=jnp.int32)
    slots = jnp.sum(jnp.where(rank[:, None, :] == ids[None, :, None], local[:, None, :], 0), axis=2)

    sources = lax.dynamic_slice_in_dim(perm, base, rows)
    owner = sources // rows
    ids_dev = jnp.arange(count, dtype=jnp.int32)
    from_dev = owner[None, :] == ids_dev[:, None]
    place = jnp.dot(from_dev.astype(jnp.bfloat16), earlier, preferred_element_type=jnp.float32).astype(jnp.int32)
    place = jnp.sum(jnp.where(from_dev, place, 0), axis=0)
    return slots.reshape(-1), owner, place


def pack_kernel(count, limit, slots_ref, b_ref, out_ref):
    def one(dest, k):
        row = slots_ref[dest * limit + k]
        out_ref[dest, pl.ds(k, 1), :] = b_ref[pl.ds(row, 1), :]

    step = min(UNROLL, limit)

    @pl.loop(0, count)
    def _(dest):
        @pl.loop(0, limit // step)
        def _(group):
            for u in range(step):
                one(dest, group * step + u)

        for k in range(limit // step * step, limit):
            one(dest, k)


def pack(matrix, slots, count, limit, first, tiles):
    rows, columns = matrix.shape
    return pl.pallas_call(
        functools.partial(pack_kernel, count, limit),
        out_shape=jax.ShapeDtypeStruct((count, limit, tiles * LANES), matrix.dtype),
        grid_spec=pltpu.PrefetchScalarGridSpec(
            num_scalar_prefetch=1,
            grid=(tiles,),
            in_specs=[pl.BlockSpec((rows, LANES), lambda t, s: (0, first + t))],
            out_specs=pl.BlockSpec((count, limit, LANES), lambda t, s: (0, 0, t)),
        ),
        cost_estimate=pl.CostEstimate(flops=0, bytes_accessed=4 * rows * tiles * LANES * 4, transcendentals=0),
        name="pack_rows",
    )(slots, matrix)


def unpack_kernel(rows, owner_ref, place_ref, got_ref, a_ref, *rest):
    out_ref = rest[-1]
    step = 16 if rows % 16 == 0 else 1

    @pl.loop(0, rows // step)
    def _(group):
        for u in range(step):
            j = group * step + u
            value = got_ref[owner_ref[j], pl.ds(place_ref[j], 1), :]
            out_ref[pl.ds(j, 1), :] = (a_ref[pl.ds(j, 1), :] + value) * 0.5


def unpack(got, own, owner, place, first, so_far):
    count, limit, width = got.shape
    rows, columns = own.shape
    tiles = width // LANES
    operands = [owner, place, got, own]
    in_specs = [
        pl.BlockSpec((count, limit, LANES), lambda t, o, p: (0, 0, t)),
        pl.BlockSpec((rows, LANES), lambda t, o, p: (0, first + t)),
    ]
    aliases = {}
    if so_far is not None:
        operands.append(so_far)
        in_specs.append(pl.BlockSpec(memory_space=pl.ANY))
        aliases = {4: 0}
    return pl.pallas_call(
        functools.partial(unpack_kernel, rows),
        out_shape=jax.ShapeDtypeStruct(own.shape, own.dtype),
        grid_spec=pltpu.PrefetchScalarGridSpec(
            num_scalar_prefetch=2,
            grid=(tiles,),
            in_specs=in_specs,
            out_specs=pl.BlockSpec((rows, LANES), lambda t, o, p: (0, first + t)),
        ),
        input_output_aliases=aliases,
        cost_estimate=pl.CostEstimate(flops=0, bytes_accessed=5 * rows * width * 4, transcendentals=0),
        name="merge_rows",
    )(*operands)


def on_device(widths, a_up, a_down, b_up, b_down, perm):
    count = lax.axis_size("units")
    me = lax.axis_index("units")
    rows, columns = b_up.shape
    limit = (rows + count - 1) // count + 1
    slots, owner, place = index_lists(perm, rows, count, limit, me)
    pieces = [("up", first, width) for first, width in widths(columns)]
    pieces += [("down", first, width) for first, width in reversed_order(widths(columns))]
    a = {"up": a_up, "down": a_down}
    b = {"up": b_up, "down": b_down}
    out = {"up": None, "down": None}
    gots = []
    for name, first, tiles in pieces:
        packed = pack(b[name], slots, count, limit, first, tiles)
        gots.append(lax.all_to_all(packed, "units", split_axis=0, concat_axis=0, tiled=True))
    for (name, first, tiles), got in zip(pieces, gots):
        out[name] = unpack(got, a[name], owner, place, first, out[name])
    return out["up"], out["down"]


def widths(columns):
    total = columns // LANES
    first = max(total // 4, 1)
    return ((0, first), (first, total - first))


def reversed_order(parts):
    total = sum(width for _, width in parts)
    return tuple((total - first - width, width) for first, width in reversed(parts))


def solution(mesh):
    split = P(("expert", "units"), None)
    return jax.shard_map(
        functools.partial(on_device, widths),
        mesh=mesh,
        in_specs=(split, split, split, split, P("expert")),
        out_specs=(split, split),
        check_vma=False,
    )
```

time: 824 us -> 772 us (0.937)
  Pallas kernels: 0 us -> 270 us
  waiting for transfers between devices: 611 us -> 469 us
  local copies, waits for them, and re-layouts: 129 us -> 0.83 us
  other arithmetic: 69.8 us -> 6.4 us
  starting transfers between devices: 12.9 us -> 22.3 us
    pallas_call x0 -> x8, Pallas kernels: none -> 270 us  [the longest x4 144 us: unpack(): pl.pallas_call(functools.partial(unpack_kernel, rows), out_shape=jax.Shap...]
    all_to_all x2 -> x4, waiting for transfers between devices: 611 us -> 469 us  [on_device(): lax.all_to_all(packed, 'units', split_axis=0, concat_axis=0, tiled=True)]
    gather x4 -> x0, local copies, waits for them, and re-layouts: 80.2 us -> none  [the longest x2 41.2 us: pack(): return jnp.take(matrix, slots, axis=0, mode='fill', fill_value=0.0)]
    all_to_all x4 -> x0, local copies, waits for them, and re-layouts: 49.3 us -> none  [the longest x2 24.7 us: on_device(): lax.all_to_all(pack(b_down), 'units', split_axis=0, concat_axis=0, tiled=...]
    mul x1 -> x0, other arithmetic: 29.7 us -> none  [unpack(): return (own + jnp.take(received, picks, axis=0)) * 0.5]
    select_n x6 -> x2, other arithmetic: 21.4 us -> 0.81 us  [the longest x1 0.8 us: index_lists(): owner = sources // rows]
    reduce_sum x4 -> x1, other arithmetic: 18.7 us -> 3.93 us  [index_lists(): jnp.sum(jnp.where(rank[:, None, :] == ids[None, :, None], local[:, None,...]
    all_to_all x2 -> x4, starting transfers between devices: 12.9 us -> 22.3 us  [on_device(): lax.all_to_all(packed, 'units', split_axis=0, concat_axis=0, tiled=True)]
  transfers between devices with their start and end apart: 2 -> 4, of which waited for: 2 -> 3; matrix products, arithmetic and copies ran while one was open for 3% -> 0% of each run, Pallas kernels for 0% -> 30%
where the time goes in v1:
time: 772 us; the launch traced here: 771 us
  waiting for transfers between devices  469 us (61%)
  Pallas kernels  270 us (35%)
  starting transfers between devices  22.3 us (3%)
    all_to_all x4, waiting for transfers between devices, on_device(): lax.all_to_all(packed, 'units', split_axis=0, concat_axis=0, tiled=True)  469 us
    pallas_call x4, Pallas kernels, unpack(): pl.pallas_call(functools.partial(unpack_kernel, rows), out_shape=jax.Shap...  144 us
    pallas_call x4, Pallas kernels, pack(): pl.pallas_call(functools.partial(pack_kernel, count, limit), out_shape=ja...  127 us
    all_to_all x4, starting transfers between devices, on_device(): lax.all_to_all(packed, 'units', split_axis=0, concat_axis=0, tiled=True)  22.3 us
  transfers between devices with their start and end apart: 4, of which 3 were waited for; matrix products, arithmetic and copies ran while one was open for 0% of the time, Pallas kernels for 30%

profile of v1, /device:TPU:0, one launch (start us, length us, event | category | flops | bytes accessed | tf_op | source)
XLA Modules:
  0.0 771.3 jit_solution(17277619516427221054)
XLA Ops:
  0.6 0.8 broadcast_subtract_fusion
  1.5 0.8 compare_and_fusion
  2.3 0.1 and.17
  2.4 0.7 fusion.5
  3.1 3.9 select_reduce_fusion
  7.0 0.1 copy.9
  7.1 0.7 reshape.32.slots_ref
  7.7 17.6 %pack_rows.5 = f32[8,225,512]{2,1,0:T(8,128)} custom-call(s32[1800]{0:T(1024)} %reshape.32.slots_ref, f32[1792,2048]{1,0:T(8,128)} %b_ref.5), custom_call_target="tpu_custom_call" | custom-call | bytes 14680064 | tf_op jit(solution)/shard_map/pack_rows/pallas_call | solution.py:55
  25.3 7.3 all-to-all-start.1
  32.6 45.7 %pack_rows.4 = f32[8,225,1536]{2,1,0:T(8,128)} custom-call(s32[1800]{0:T(1024)} %reshape.32.slots_ref, f32[1792,2048]{1,0:T(8,128)} %b_ref.5), custom_call_target="tpu_custom_call" | custom-call | bytes 44040192 | tf_op jit(solution)/shard_map/pack_rows/pallas_call | solution.py:55
  78.3 39.1 %all-to-all-done.1.got_ref = f32[8,225,512]{2,1,0:T(8,128)} async-done(((f32[8,225,512]{2,1,0:T(8,128)}), f32[8,225,512]{2,1,0:T(8,128)}, u32[]{:S(2)}, u32[]{:S(2)}) %all-to-all-start.1) | async-done | bytes 3686432 | tf_op jit(solution)/shard_map/all_to_all | solution.py:124
  117.4 5.3 all-to-all-start
  122.7 45.7 %pack_rows.7 = f32[8,225,1536]{2,1,0:T(8,128)} custom-call(s32[1800]{0:T(1024)} %reshape.32.slots_ref, f32[1792,2048]{1,0:T(8,128)} %b_ref.7), custom_call_target="tpu_custom_call" | custom-call | bytes 44040192 | tf_op jit(solution)/shard_map/pack_rows/pallas_call | solution.py:55
  168.4 201.2 %all-to-all-done.got_ref = f32[8,225,1536]{2,1,0:T(8,128)} async-done(((f32[8,225,1536]{2,1,0:T(8,128)}), f32[8,225,1536]{2,1,0:T(8,128)}, u32[]{:S(2)}, u32[]{:S(2)}) %all-to-all-start) | async-done | bytes 11059232 | tf_op jit(solution)/shard_map/all_to_all | solution.py:124
  369.6 5.2 all-to-all-start.3
  374.8 17.6 %pack_rows.6 = f32[8,225,512]{2,1,0:T(8,128)} custom-call(s32[1800]{0:T(1024)} %reshape.32.slots_ref, f32[1792,2048]{1,0:T(8,128)} %b_ref.7), custom_call_target="tpu_custom_call" | custom-call | bytes 14680064 | tf_op jit(solution)/shard_map/pack_rows/pallas_call | solution.py:55
  392.4 228.7 %all-to-all-done.3.got_ref = f32[8,225,1536]{2,1,0:T(8,128)} async-done(((f32[8,225,1536]{2,1,0:T(8,128)}), f32[8,225,1536]{2,1,0:T(8,128)}, u32[]{:S(2)}, u32[]{:S(2)}) %all-to-all-start.3) | async-done | bytes 11059232 | tf_op jit(solution)/shard_map/all_to_all | solution.py:124
  621.1 4.5 all-to-all-start.2
  625.6 0.8 add_select_fusion.owner_ref
  626.4 0.0 copy-start
  626.4 1.3 fusion.6.place_ref
  627.7 0.0 copy-done
  627.7 20.0 %merge_rows.4.rest_0_ = f32[1792,2048]{1,0:T(8,128)} custom-call(s32[1792]{0:T(1024)} %copy-done, s32[1792]{0:T(1024)} %fusion.6.place_ref, f32[8,225,512]{2,1,0:T(8,128)} %all-to-all-done.1.got_ref, f32[1792,2048]{1,0:T(8,128)} %a_ref.5), custom_call_target="tpu_custom_call" | custom-call | bytes 18350080 | tf_op jit(solution)/shard_map/merge_rows/pallas_call | solution.py:95
  647.7 51.8 %merge_rows.5 = f32[1792,2048]{1,0:T(8,128)} custom-call(s32[1792]{0:T(1024)} %copy-done, s32[1792]{0:T(1024)} %fusion.6.place_ref, f32[8,225,1536]{2,1,0:T(8,128)} %all-to-all-done.got_ref, f32[1792,2048]{1,0:T(8,128)} %a_ref.5, f32[1792,2048]{1,0:T(8,128)} %merge_rows.4.rest_0_), custom_call_target="tpu_custom_call", output_to_operand_aliasing={{}: (4, {})} | custom-call | bytes 55050240 | tf_op jit(solution)/shard_map/merge_rows/pallas_call | solution.py:95
  699.5 51.8 %merge_rows.6.rest_0_ = f32[1792,2048]{1,0:T(8,128)} custom-call(s32[1792]{0:T(1024)} %copy-done, s32[1792]{0:T(1024)} %fusion.6.place_ref, f32[8,225,1536]{2,1,0:T(8,128)} %all-to-all-done.3.got_ref, f32[1792,2048]{1,0:T(8,128)} %a_ref.7), custom_call_target="tpu_custom_call" | custom-call | bytes 55050240 | tf_op jit(solution)/shard_map/merge_rows/pallas_call | solution.py:95
  751.2 0.0 all-to-all-done.2.got_ref
  751.2 20.0 %merge_rows.7 = f32[1792,2048]{1,0:T(8,128)} custom-call(s32[1792]{0:T(1024)} %copy-done, s32[1792]{0:T(1024)} %fusion.6.place_ref, f32[8,225,512]{2,1,0:T(8,128)} %all-to-all-done.2.got_ref, f32[1792,2048]{1,0:T(8,128)} %a_ref.7, f32[1792,2048]{1,0:T(8,128)} %merge_rows.6.rest_0_), custom_call_target="tpu_custom_call", output_to_operand_aliasing={{}: (4, {})} | custom-call | bytes 18350080 | tf_op jit(solution)/shard_map/merge_rows/pallas_call | solution.py:95
  (2 shorter events, 0.0 us)
Async XLA Ops:
  25.3 92.1 %all-to-all-start.1 = ((f32[8,225,512]{2,1,0:T(8,128)}), f32[8,225,512]{2,1,0:T(8,128)}, u32[]{:S(2)}, u32[]{:S(2)}) async-start(f32[8,225,512]{2,1,0:T(8,128)} %pack_rows.5), calls=%async_computation.1 | async-start | bytes 7602176 | tf_op jit(solution)/shard_map/all_to_all | solution.py:124
  117.4 252.1 %all-to-all-start = ((f32[8,225,1536]{2,1,0:T(8,128)}), f32[8,225,1536]{2,1,0:T(8,128)}, u32[]{:S(2)}, u32[]{:S(2)}) async-start(f32[8,225,1536]{2,1,0:T(8,128)} %pack_rows.4), calls=%async_computation | async-start | bytes 22806528 | tf_op jit(solution)/shard_map/all_to_all | solution.py:124
  369.6 251.5 %all-to-all-start.3 = ((f32[8,225,1536]{2,1,0:T(8,128)}), f32[8,225,1536]{2,1,0:T(8,128)}, u32[]{:S(2)}, u32[]{:S(2)}) async-start(f32[8,225,1536]{2,1,0:T(8,128)} %pack_rows.7), calls=%async_computation.3 | async-start | bytes 22806528 | tf_op jit(solution)/shard_map/all_to_all | solution.py:124
  621.1 130.2 %all-to-all-start.2 = ((f32[8,225,512]{2,1,0:T(8,128)}), f32[8,225,512]{2,1,0:T(8,128)}, u32[]{:S(2)}, u32[]{:S(2)}) async-start(f32[8,225,512]{2,1,0:T(8,128)} %pack_rows.6), calls=%async_computation.2 | async-start | bytes 7602176 | tf_op jit(solution)/shard_map/all_to_all | solution.py:124
  626.4 1.3 copy-start

commit v2 on v1

v2 whole, which is shorter than its diff:
```python
import functools

import jax
import jax.numpy as jnp
from jax import lax
from jax.experimental import pallas as pl
from jax.experimental.pallas import tpu as pltpu
from jax.sharding import PartitionSpec as P


LANES = 512
BATCH = 8


def peers(count):
    return [(count - p) % count for p in range(count)]


def index_lists(perm, rows, count, limit, me):
    base = me * rows
    table = perm.reshape(count, rows)
    mine = (table >= base) & (table < base + rows)
    upto = jnp.arange(rows, dtype=jnp.int32)
    earlier = (upto[:, None] < upto[None, :]).astype(jnp.bfloat16)
    rank = jnp.dot(mine.astype(jnp.bfloat16), earlier, preferred_element_type=jnp.float32).astype(jnp.int32)
    rank = jnp.where(mine, rank, -1)
    local = jnp.where(mine, table - base, 0)
    ids = jnp.arange(limit, dtype=jnp.int32)
    slots = jnp.sum(jnp.where(rank[:, None, :] == ids[None, :, None], local[:, None, :], 0), axis=2)

    sources = lax.dynamic_slice_in_dim(perm, base, rows)
    owner = sources // rows
    ids_dev = jnp.arange(count, dtype=jnp.int32)
    from_dev = owner[None, :] == ids_dev[:, None]
    place = jnp.dot(from_dev.astype(jnp.bfloat16), earlier, preferred_element_type=jnp.float32).astype(jnp.int32)
    place = jnp.sum(jnp.where(from_dev, place, 0), axis=0)
    padded = (limit + 7) // 8 * 8
    place_of = (count - (owner ^ me)) % count
    return slots.reshape(-1), place_of * padded + place


def pack_kernel(count, limit, slots_ref, me_ref, b_ref, *out_refs):
    def some(out_ref, base, first, size):
        values = [b_ref[pl.ds(slots_ref[base + first + u], 1), :] for u in range(size)]
        for u in range(size):
            out_ref[pl.ds(first + u, 1), :] = values[u]

    for out_ref, k in zip(out_refs, peers(count)):
        base = (me_ref[0] ^ k) * limit

        @pl.loop(0, limit // BATCH)
        def _(group):
            some(out_ref, base, pl.multiple_of(group * BATCH, BATCH), BATCH)

        if limit % BATCH:
            some(out_ref, base, limit // BATCH * BATCH, limit % BATCH)


def pack(matrix, slots, me, count, limit, first, tiles):
    rows, _ = matrix.shape
    return pl.pallas_call(
        functools.partial(pack_kernel, count, limit),
        out_shape=[jax.ShapeDtypeStruct((limit, tiles * LANES), matrix.dtype)] * count,
        grid_spec=pltpu.PrefetchScalarGridSpec(
            num_scalar_prefetch=2,
            grid=(tiles,),
            in_specs=[pl.BlockSpec((rows, LANES), lambda t, s, m: (0, first + t))],
            out_specs=[pl.BlockSpec((limit, LANES), lambda t, s, m: (0, t))] * count,
        ),
        cost_estimate=pl.CostEstimate(flops=0, bytes_accessed=4 * rows * tiles * LANES * 4, transcendentals=0),
        name="pack_rows",
    )(slots, me.reshape(1), matrix)


def merge_kernel(count, limit, picks_ref, *refs):
    got_refs, a_ref, out_ref, table = refs[:count], refs[count], refs[-2], refs[-1]
    rows = a_ref.shape[0]
    padded = table.shape[0] // count
    for k in range(count):
        table[pl.ds(k * padded, limit), :] = got_refs[k][...]

    @pl.loop(0, rows // BATCH)
    def _(group):
        first = pl.multiple_of(group * BATCH, BATCH)
        values = [table[pl.ds(picks_ref[first + u], 1), :] for u in range(BATCH)]
        owns = [a_ref[pl.ds(first + u, 1), :] for u in range(BATCH)]
        for u in range(BATCH):
            out_ref[pl.ds(first + u, 1), :] = (owns[u] + values[u]) * 0.5


def merge(gots, own, picks, first, so_far):
    count = len(gots)
    limit, width = gots[0].shape
    rows, _ = own.shape
    tiles = width // LANES
    padded = (limit + 7) // 8 * 8
    operands = [picks, *gots, own]
    in_specs = [pl.BlockSpec((limit, LANES), lambda t, p: (0, t))] * count
    in_specs.append(pl.BlockSpec((rows, LANES), lambda t, p: (0, first + t)))
    aliases = {}
    if so_far is not None:
        aliases = {len(operands): 0}
        operands.append(so_far)
        in_specs.append(pl.BlockSpec(memory_space=pl.ANY))
    return pl.pallas_call(
        functools.partial(merge_kernel, count, limit),
        out_shape=jax.ShapeDtypeStruct(own.shape, own.dtype),
        grid_spec=pltpu.PrefetchScalarGridSpec(
            num_scalar_prefetch=1,
            grid=(tiles,),
            in_specs=in_specs,
            out_specs=pl.BlockSpec((rows, LANES), lambda t, p: (0, first + t)),
            scratch_shapes=[pltpu.VMEM((count * padded, LANES), own.dtype)],
        ),
        input_output_aliases=aliases,
        cost_estimate=pl.CostEstimate(flops=0, bytes_accessed=6 * rows * width * 4, transcendentals=0),
        name="merge_rows",
    )(*operands)


def exchange(parts, count, me):
    order = peers(count)
    if count <= 8:
        got = [lax.ppermute(part, "units", [(i, i ^ k) for i in range(count)]) for part, k in zip(parts[1:], order[1:])]
        return [parts[0], *got]
    places = (count - (jnp.arange(count, dtype=jnp.int32) ^ me)) % count
    back = lax.all_to_all(jnp.take(jnp.stack(parts), places, axis=0), "units", split_axis=0, concat_axis=0, tiled=True)
    back = jnp.take(back, jnp.array(order, jnp.int32) ^ me, axis=0)
    return [back[k] for k in range(count)]


def pieces_of(columns):
    total = columns // LANES
    sizes = [1, 1, total - 2] if total > 2 else [total]
    plan = []
    for which, widths in ((0, sizes), (1, sizes[::-1])):
        first = 0
        for tiles in widths:
            plan.append((which, first, tiles))
            first += tiles
    return plan


def on_device(a_up, a_down, b_up, b_down, perm):
    count = lax.axis_size("units")
    me = lax.axis_index("units")
    rows, columns = b_up.shape
    limit = (rows + count - 1) // count + 1
    slots, picks = index_lists(perm, rows, count, limit, me)
    own, other, out = (a_up, a_down), (b_up, b_down), [None, None]
    gots = []
    plan = pieces_of(columns)
    for at, (which, first, tiles) in enumerate(plan):
        parts = pack(other[which], slots, me, count, limit, first, tiles)
        slots, parts = lax.optimization_barrier((slots, parts))
        if at >= 3:
            parts, gots[at - 3] = lax.optimization_barrier((parts, gots[at - 3]))
        gots.append(exchange(parts, count, me))
    for at, (which, first, tiles) in enumerate(plan):
        merged = merge(gots[at], own[which], picks, first, out[which])
        picks, out[which] = lax.optimization_barrier((picks, merged))
    return out[0], out[1]


def solution(mesh):
    split = P(("expert", "units"), None)
    return jax.shard_map(
        on_device,
        mesh=mesh,
        in_specs=(split, split, split, split, P("expert")),
        out_specs=(split, split),
        check_vma=False,
    )
```

time: 772 us -> 773 us (level)
  starting transfers between devices: 22.3 us -> 380 us
  waiting for transfers between devices: 469 us -> 196 us
  Pallas kernels: 270 us -> 178 us
    all_to_all x4 -> x0, waiting for transfers between devices: 469 us -> none  [on_device(): lax.all_to_all(packed, 'units', split_axis=0, concat_axis=0, tiled=True)]
    ppermute x0 -> x42, starting transfers between devices: none -> 380 us  [exchange(): lax.ppermute(part, 'units', [(i, i ^ k) for i in range(count)])]
    ppermute x0 -> x42, waiting for transfers between devices: none -> 196 us  [exchange(): lax.ppermute(part, 'units', [(i, i ^ k) for i in range(count)])]
    pallas_call x8 -> x12, Pallas kernels: 270 us -> 178 us  [the longest x6 95 us: merge(): pl.pallas_call(functools.partial(merge_kernel, count, limit), out_shape=j...]
    all_to_all x4 -> x0, starting transfers between devices: 22.3 us -> none  [on_device(): lax.all_to_all(packed, 'units', split_axis=0, concat_axis=0, tiled=True)]
  transfers between devices with their start and end apart: 4 -> 42, of which waited for: 3 -> 16; matrix products, arithmetic and copies ran while one was open for 0% -> 0% of each run, Pallas kernels for 30% -> 20%
where the time goes in v2:
time: 773 us; the launch traced here: 766 us
  starting transfers between devices  380 us (49%)
  waiting for transfers between devices  196 us (25%)
  Pallas kernels  178 us (23%)
  other arithmetic  7.8 us (1%)
    ppermute x42, starting transfers between devices, exchange(): lax.ppermute(part, 'units', [(i, i ^ k) for i in range(count)])  380 us
    ppermute x42, waiting for transfers between devices, exchange(): lax.ppermute(part, 'units', [(i, i ^ k) for i in range(count)])  196 us
    pallas_call x6, Pallas kernels, merge(): pl.pallas_call(functools.partial(merge_kernel, count, limit), out_shape=j...  95 us
    pallas_call x6, Pallas kernels, pack(): pl.pallas_call(functools.partial(pack_kernel, count, limit), out_shape=[j...  83.3 us
  transfers between devices with their start and end apart: 42, of which 16 were waited for; matrix products, arithmetic and copies ran while one was open for 0% of the time, Pallas kernels for 20%

profile of v2, /device:TPU:0, one launch (start us, length us, event | category | flops | bytes accessed | tf_op | source)
XLA Modules:
  0.0 766.5 jit_solution(16002011900368775292)
XLA Ops:
  3.1 3.9 select_reduce_fusion
  7.8 11.5 %pack_rows.6 = (f32[225,512]{1,0:T(8,128)}, f32[225,512]{1,0:T(8,128)}, f32[225,512]{1,0:T(8,128)}, f32[225,512]{1,0:T(8,128)}, f32[225,512]{1,0:T(8,128)}, /*in...) custom-call(s32[1800]{0:T(1024)} %reshape.40.slots_ref, s32[1]{0:T(128)} %bitcast.me_ref, f32[1792,2048]{1,0:T(8,128)} %b_ref.8), custom_call_target="tpu_custom_call" | custom-call | bytes 14680064 | tf_op jit(solution)/shard_map/pack_rows/pallas_call | solution.py:61
  19.3 6.0 collective-permute-start
  30.6 6.9 collective-permute-done.refs_1_
  37.5 47.3 %collective-permute-start.5 = (f32[225,512]{1,0:T(8,128)}, f32[225,512]{1,0:T(8,128)S(1)}, u32[]{:S(2)}, u32[]{:S(2)}) collective-permute-start(f32[225,512]{1,0:T(8,128)} %get-tuple-element.211), channel_id=1, source_target_pairs={{0,8},{4,12},{8,0},{12,4},{16,24},{20,28},{24,16},{28,20},{1,9},{5... | collective-permute-start | bytes 1382408 | tf_op jit(solution)/shard_map/ppermute | solution.py:124
  84.9 11.6 %pack_rows.7 = (f32[225,512]{1,0:T(8,128)}, f32[225,512]{1,0:T(8,128)}, f32[225,512]{1,0:T(8,128)}, f32[225,512]{1,0:T(8,128)}, f32[225,512]{1,0:T(8,128)}, /*in...) custom-call(s32[1800]{0:T(1024)} %reshape.40.slots_ref, s32[1]{0:T(128)} %bitcast.me_ref, f32[1792,2048]{1,0:T(8,128)} %b_ref.8), custom_call_target="tpu_custom_call" | custom-call | bytes 14680064 | tf_op jit(solution)/shard_map/pack_rows/pallas_call | solution.py:61
  97.9 5.8 collective-permute-done.2.refs_3_
  103.7 3.2 collective-permute-start.7
  106.9 17.0 %collective-permute-done.3.refs_4_ = f32[225,512]{1,0:T(8,128)S(1)} collective-permute-done((f32[225,512]{1,0:T(8,128)}, f32[225,512]{1,0:T(8,128)S(1)}, u32[]{:S(2)}, u32[]{:S(2)}) %collective-permute-start.3) | collective-permute-done | bytes 460832 | tf_op jit(solution)/shard_map/ppermute | solution.py:124
  126.4 2.9 collective-permute-start.10
  129.4 18.5 %pack_rows.8 = (f32[225,1024]{1,0:T(8,128)}, f32[225,1024]{1,0:T(8,128)}, f32[225,1024]{1,0:T(8,128)}, f32[225,1024]{1,0:T(8,128)}, f32[225,1024]{1,0:T(8,128)},...) custom-call(s32[1800]{0:T(1024)} %reshape.40.slots_ref, s32[1]{0:T(128)} %bitcast.me_ref, ...), custom_call_target="tpu_custom_call" | custom-call | bytes 29360128 | tf_op jit(solution)/shard_map/pack_rows/pallas_call | solution.py:61
  147.9 2.4 collective-permute-start.14
  152.7 63.5 %collective-permute-start.11 = (f32[225,512]{1,0:T(8,128)}, f32[225,512]{1,0:T(8,128)S(1)}, u32[]{:S(2)}, u32[]{:S(2)}) collective-permute-start(f32[225,512]{1,0:T(8,128)} %get-tuple-element.244), channel_id=1, source_target_pairs={{0,12},{4,8},{8,4},{12,0},{16,28},{20,24},{24,20},{28,16},{1,13},{... | collective-permute-start | bytes 1382408 | tf_op jit(solution)/shard_map/ppermute | solution.py:124
  216.2 9.7 %collective-permute-done.9.refs_3_ = f32[225,512]{1,0:T(8,128)S(1)} collective-permute-done((f32[225,512]{1,0:T(8,128)}, f32[225,512]{1,0:T(8,128)S(1)}, u32[]{:S(2)}, u32[]{:S(2)}) %collective-permute-start.9) | collective-permute-done | bytes 460832 | tf_op jit(solution)/shard_map/ppermute | solution.py:124
  226.0 10.0 %collective-permute-done.10.refs_4_ = f32[225,512]{1,0:T(8,128)S(1)} collective-permute-done((f32[225,512]{1,0:T(8,128)}, f32[225,512]{1,0:T(8,128)S(1)}, u32[]{:S(2)}, u32[]{:S(2)}) %collective-permute-start.10) | collective-permute-done | bytes 460832 | tf_op jit(solution)/shard_map/ppermute | solution.py:124
  236.6 8.7 %collective-permute-done.11.refs_5_ = f32[225,512]{1,0:T(8,128)S(1)} collective-permute-done((f32[225,512]{1,0:T(8,128)}, f32[225,512]{1,0:T(8,128)S(1)}, u32[]{:S(2)}, u32[]{:S(2)}) %collective-permute-start.11) | collective-permute-done | bytes 460832 | tf_op jit(solution)/shard_map/ppermute | solution.py:124
  246.2 9.3 %collective-permute-done.12.refs_6_ = f32[225,512]{1,0:T(8,128)S(1)} collective-permute-done((f32[225,512]{1,0:T(8,128)}, f32[225,512]{1,0:T(8,128)S(1)}, u32[]{:S(2)}, u32[]{:S(2)}) %collective-permute-start.12) | collective-permute-done | bytes 460832 | tf_op jit(solution)/shard_map/ppermute | solution.py:124
  256.2 23.3 %collective-permute-start.18 = (f32[225,1024]{1,0:T(8,128)}, f32[225,1024]{1,0:T(8,128)S(1)}, u32[]{:S(2)}, u32[]{:S(2)}) collective-permute-start(f32[225,1024]{1,0:T(8,128)} %get-tuple-element.279), channel_id=1, source_target_pairs={{0,12},{4,8},{8,4},{12,0},{16,28},{20,24},{24,20},{28,16},{1,13},{... | collective-permute-start | bytes 2764808 | tf_op jit(solution)/shard_map/ppermute | solution.py:124
  279.5 22.9 %collective-permute-start.19 = (f32[225,1024]{1,0:T(8,128)}, f32[225,1024]{1,0:T(8,128)}, u32[]{:S(2)}, u32[]{:S(2)}) collective-permute-start(f32[225,1024]{1,0:T(8,128)} %get-tuple-element.280), channel_id=1, source_target_pairs={{0,8},{4,12},{8,0},{12,4},{16,24},{20,28},{24,16},{28,20},{1,9},{5... | collective-permute-start | bytes 2764808 | tf_op jit(solution)/shard_map/ppermute | solution.py:124
  304.8 18.5 %pack_rows.9 = (f32[225,1024]{1,0:T(8,128)}, f32[225,1024]{1,0:T(8,128)}, f32[225,1024]{1,0:T(8,128)}, f32[225,1024]{1,0:T(8,128)}, f32[225,1024]{1,0:T(8,128)},...) custom-call(s32[1800]{0:T(1024)} %reshape.40.slots_ref, s32[1]{0:T(128)} %bitcast.me_ref, ...), custom_call_target="tpu_custom_call" | custom-call | bytes 29360128 | tf_op jit(solution)/shard_map/pack_rows/pallas_call | solution.py:61
  323.3 11.6 %pack_rows.10 = (f32[225,512]{1,0:T(8,128)}, f32[225,512]{1,0:T(8,128)}, f32[225,512]{1,0:T(8,128)}, f32[225,512]{1,0:T(8,128)}, f32[225,512]{1,0:T(8,128)}, /*i...) custom-call(s32[1800]{0:T(1024)} %reshape.40.slots_ref, s32[1]{0:T(128)} %bitcast.me_ref, f32[1792,2048]{1,0:T(8,128)} %b_ref.11), custom_call_target="tpu_custom_call" | custom-call | bytes 14680064 | tf_op jit(solution)/shard_map/pack_rows/pallas_call | solution.py:61
  334.9 6.7 collective-permute-done.16.refs_3_
  341.6 4.2 collective-permute-start.28
  345.8 27.2 %collective-permute-done.17.refs_4_ = f32[225,1024]{1,0:T(8,128)S(1)} collective-permute-done((f32[225,1024]{1,0:T(8,128)}, f32[225,1024]{1,0:T(8,128)S(1)}, u32[]{:S(2)}, u32[]{:S(2)}) %collective-permute-start.17) | collective-permute-done | bytes 921632 | tf_op jit(solution)/shard_map/ppermute | solution.py:124
  377.3 3.3 collective-permute-start.21
  380.7 2.4 collective-permute-start.22
  383.1 5.7 collective-permute-done.29.refs_2_
  388.8 75.5 %collective-permute-start.32 = (f32[225,512]{1,0:T(8,128)}, f32[225,512]{1,0:T(8,128)S(1)}, u32[]{:S(2)}, u32[]{:S(2)}) collective-permute-start(f32[225,512]{1,0:T(8,128)} %get-tuple-element.307), channel_id=1, source_target_pairs={{0,12},{4,8},{8,4},{12,0},{16,28},{20,24},{24,20},{28,16},{1,13},{... | collective-permute-start | bytes 1382408 | tf_op jit(solution)/shard_map/ppermute | solution.py:124
  464.3 9.7 %collective-permute-done.30.refs_3_ = f32[225,512]{1,0:T(8,128)S(1)} collective-permute-done((f32[225,512]{1,0:T(8,128)}, f32[225,512]{1,0:T(8,128)S(1)}, u32[]{:S(2)}, u32[]{:S(2)}) %collective-permute-start.30) | collective-permute-done | bytes 460832 | tf_op jit(solution)/shard_map/ppermute | solution.py:124
  474.5 10.5 %collective-permute-done.31.refs_4_ = f32[225,512]{1,0:T(8,128)S(1)} collective-permute-done((f32[225,512]{1,0:T(8,128)}, f32[225,512]{1,0:T(8,128)S(1)}, u32[]{:S(2)}, u32[]{:S(2)}) %collective-permute-start.31) | collective-permute-done | bytes 460832 | tf_op jit(solution)/shard_map/ppermute | solution.py:124
  485.0 8.4 %collective-permute-done.32.refs_5_ = f32[225,512]{1,0:T(8,128)S(1)} collective-permute-done((f32[225,512]{1,0:T(8,128)}, f32[225,512]{1,0:T(8,128)S(1)}, u32[]{:S(2)}, u32[]{:S(2)}) %collective-permute-start.32) | collective-permute-done | bytes 460832 | tf_op jit(solution)/shard_map/ppermute | solution.py:124
  493.8 10.7 %collective-permute-done.33.refs_6_ = f32[225,512]{1,0:T(8,128)S(1)} collective-permute-done((f32[225,512]{1,0:T(8,128)}, f32[225,512]{1,0:T(8,128)S(1)}, u32[]{:S(2)}, u32[]{:S(2)}) %collective-permute-start.33) | collective-permute-done | bytes 460832 | tf_op jit(solution)/shard_map/ppermute | solution.py:124
  504.6 23.7 %collective-permute-start.25 = (f32[225,1024]{1,0:T(8,128)}, f32[225,1024]{1,0:T(8,128)}, u32[]{:S(2)}, u32[]{:S(2)}) collective-permute-start(f32[225,1024]{1,0:T(8,128)} %get-tuple-element.298), channel_id=1, source_target_pairs={{0,12},{4,8},{8,4},{12,0},{16,28},{20,24},{24,20},{28,16},{1,13},{... | collective-permute-start | bytes 2764808 | tf_op jit(solution)/shard_map/ppermute | solution.py:124
  528.3 23.0 %collective-permute-start.26 = (f32[225,1024]{1,0:T(8,128)}, f32[225,1024]{1,0:T(8,128)}, u32[]{:S(2)}, u32[]{:S(2)}) collective-permute-start(f32[225,1024]{1,0:T(8,128)} %get-tuple-element.299), channel_id=1, source_target_pairs={{0,8},{4,12},{8,0},{12,4},{16,24},{20,28},{24,16},{28,20},{1,9},{5... | collective-permute-start | bytes 2764808 | tf_op jit(solution)/shard_map/ppermute | solution.py:124
  551.4 3.5 collective-permute-start.27
  554.9 11.6 %pack_rows.11 = (f32[225,512]{1,0:T(8,128)}, f32[225,512]{1,0:T(8,128)}, f32[225,512]{1,0:T(8,128)}, f32[225,512]{1,0:T(8,128)}, f32[225,512]{1,0:T(8,128)}, /*i...) custom-call(s32[1800]{0:T(1024)} %reshape.40.slots_ref, s32[1]{0:T(128)} %bitcast.me_ref, f32[1792,2048]{1,0:T(8,128)} %b_ref.11), custom_call_target="tpu_custom_call" | custom-call | bytes 14680064 | tf_op jit(solution)/shard_map/pack_rows/pallas_call | solution.py:61
  566.4 22.2 %collective-permute-done.23.refs_3_ = f32[225,1024]{1,0:T(8,128)S(1)} collective-permute-done((f32[225,1024]{1,0:T(8,128)}, f32[225,1024]{1,0:T(8,128)S(1)}, u32[]{:S(2)}, u32[]{:S(2)}) %collective-permute-start.23) | collective-permute-done | bytes 921632 | tf_op jit(solution)/shard_map/ppermute | solution.py:124
  588.6 7.0 collective-permute-start.35
  595.7 27.4 %collective-permute-done.24.refs_4_ = f32[225,1024]{1,0:T(8,128)} collective-permute-done((f32[225,1024]{1,0:T(8,128)}, f32[225,1024]{1,0:T(8,128)}, u32[]{:S(2)}, u32[]{:S(2)}) %collective-permute-start.24) | collective-permute-done | bytes 921632 | tf_op jit(solution)/shard_map/ppermute | solution.py:124
  625.5 13.9 %collective-permute-start.39 = (f32[225,512]{1,0:T(8,128)}, f32[225,512]{1,0:T(8,128)}, u32[]{:S(2)}, u32[]{:S(2)}) collective-permute-start(f32[225,512]{1,0:T(8,128)} %get-tuple-element.317), channel_id=1, source_target_pairs={{0,12},{4,8},{8,4},{12,0},{16,28},{20,24},{24,20},{28,16},{1,13},{... | collective-permute-start | bytes 1382408 | tf_op jit(solution)/shard_map/ppermute | solution.py:124
  639.4 25.5 %collective-permute-start.40 = (f32[225,512]{1,0:T(8,128)}, f32[225,512]{1,0:T(8,128)}, u32[]{:S(2)}, u32[]{:S(2)}) collective-permute-start(f32[225,512]{1,0:T(8,128)} %get-tuple-element.318), channel_id=1, source_target_pairs={{0,8},{4,12},{8,0},{12,4},{16,24},{20,28},{24,16},{28,20},{1,9},{5... | collective-permute-start | bytes 1382408 | tf_op jit(solution)/shard_map/ppermute | solution.py:124
  664.9 3.6 collective-permute-start.41
  671.4 13.2 %merge_rows.6.refs_9_ = f32[1792,2048]{1,0:T(8,128)} custom-call(s32[1792]{0:T(1024)} %fusion.10.picks_ref, f32[225,512]{1,0:T(8,128)} %get-tuple-element.213.refs_0_, f32[225,512]{1,0:T(8,128)} %collective-permute-done.refs_1_, f32[225,512]{1,0:T(8,128)} %copy-done.19, f32[225,512]{1,0:T(8,128)} %copy-done.20, f32[225,512]{1,0:T(8,128)} %copy-done.21, ...), custom_call_target="tpu_custom_call" | custom-call | bytes 22020096 | tf_op jit(solution)/shard_map/merge_rows/pallas_call | solution.py:105
  684.7 13.3 %merge_rows.7.refs_9_ = f32[1792,2048]{1,0:T(8,128)} custom-call(s32[1792]{0:T(1024)} %fusion.10.picks_ref, f32[225,512]{1,0:T(8,128)} %get-tuple-element.247.refs_0_, f32[225,512]{1,0:T(8,128)} %copy-done.6, f32[225,512]{1,0:T(8,128)} %copy-done.7, f32[225,512]{1,0:T(8,128)} %copy-done.8, f32[225,512]{1,0:T(8,128)} %copy-done.9, ...), custom_call_target="tpu_custom_call", output_to_operand_aliasing={{}: (10, {})} | custom-call | bytes 22020096 | tf_op jit(solution)/shard_map/merge_rows/pallas_call | solution.py:105
  697.9 21.0 %merge_rows.8 = f32[1792,2048]{1,0:T(8,128)} custom-call(s32[1792]{0:T(1024)} %fusion.10.picks_ref, f32[225,1024]{1,0:T(8,128)} %get-tuple-element.282.refs_0_, f32[225,1024]{1,0:T(8,128)} %collective-permute-done.14.refs_1_, f32[225,1024]{1,0:T(8,128)} %collective-permute-done.15.refs_2_, f32[225,1024]{1,0:T(8,128)} %copy-done.3, ...), custom_call_target="tpu_custom_call", output_to_operand_aliasing={{}: (10, {})} | custom-call | bytes 44040192 | tf_op jit(solution)/shard_map/merge_rows/pallas_call | solution.py:105
  718.9 21.0 %merge_rows.9.refs_9_ = f32[1792,2048]{1,0:T(8,128)} custom-call(s32[1792]{0:T(1024)} %fusion.10.picks_ref, f32[225,1024]{1,0:T(8,128)} %get-tuple-element.293.refs_0_, f32[225,1024]{1,0:T(8,128)} %copy-done, f32[225,1024]{1,0:T(8,128)} %copy-done.1, f32[225,1024]{1,0:T(8,128)} %copy-done.2, f32[225,1024]{1,0:T(8,128)} %collective-permute-done.24.refs_4_, ...), custom_call_target="tpu_custom_call" | custom-call | bytes 44040192 | tf_op jit(solution)/shard_map/merge_rows/pallas_call | solution.py:105
  739.9 13.2 %merge_rows.10.refs_9_ = f32[1792,2048]{1,0:T(8,128)} custom-call(s32[1792]{0:T(1024)} %fusion.10.picks_ref, f32[225,512]{1,0:T(8,128)} %get-tuple-element.302.refs_0_, f32[225,512]{1,0:T(8,128)} %copy-done.12, f32[225,512]{1,0:T(8,128)} %copy-done.13, f32[225,512]{1,0:T(8,128)} %copy-done.14, ...), custom_call_target="tpu_custom_call", output_to_operand_aliasing={{}: (10, {})} | custom-call | bytes 22020096 | tf_op jit(solution)/shard_map/merge_rows/pallas_call | solution.py:105
  753.2 13.3 %merge_rows.11 = f32[1792,2048]{1,0:T(8,128)} custom-call(s32[1792]{0:T(1024)} %fusion.10.picks_ref, f32[225,512]{1,0:T(8,128)} %get-tuple-element.312.refs_0_, f32[225,512]{1,0:T(8,128)} %collective-permute-done.35.refs_1_, f32[225,512]{1,0:T(8,128)} %collective-permute-done.36.refs_2_, ...), custom_call_target="tpu_custom_call", output_to_operand_aliasing={{}: (10, {})} | custom-call | bytes 22020096 | tf_op jit(solution)/shard_map/merge_rows/pallas_call | solution.py:105
  (110 shorter events, 30.0 us)
Async XLA Ops:
  19.3 18.2 %collective-permute-start = (f32[225,512]{1,0:T(8,128)}, f32[225,512]{1,0:T(8,128)}, u32[]{:S(2)}, u32[]{:S(2)}) collective-permute-start(f32[225,512]{1,0:T(8,128)} %get-tuple-element.206), channel_id=1, source_target_pairs={{0,28},{4,24},{8,20},{12,16},{16,12},{20,8},{24,4},{28,0},{1,29},{... | collective-permute-start | bytes 1382408 | tf_op jit(solution)/shard_map/ppermute | solution.py:124
  25.3 71.2 %collective-permute-start.1 = (f32[225,512]{1,0:T(8,128)}, f32[225,512]{1,0:T(8,128)S(1)}, u32[]{:S(2)}, u32[]{:S(2)}) collective-permute-start(f32[225,512]{1,0:T(8,128)} %get-tuple-element.207), channel_id=1, source_target_pairs={{0,24},{4,28},{8,16},{12,20},{16,8},{20,12},{24,0},{28,4},{1,25},{... | collective-permute-start | bytes 1382408 | tf_op jit(solution)/shard_map/ppermute | solution.py:124
  25.5 78.2 %collective-permute-start.2 = (f32[225,512]{1,0:T(8,128)}, f32[225,512]{1,0:T(8,128)S(1)}, u32[]{:S(2)}, u32[]{:S(2)}) collective-permute-start(f32[225,512]{1,0:T(8,128)} %get-tuple-element.208), channel_id=1, source_target_pairs={{0,20},{4,16},{8,28},{12,24},{16,4},{20,0},{24,12},{28,8},{1,21},{... | collective-permute-start | bytes 1382408 | tf_op jit(solution)/shard_map/ppermute | solution.py:124
  26.3 97.7 %collective-permute-start.3 = (f32[225,512]{1,0:T(8,128)}, f32[225,512]{1,0:T(8,128)S(1)}, u32[]{:S(2)}, u32[]{:S(2)}) collective-permute-start(f32[225,512]{1,0:T(8,128)} %get-tuple-element.209), channel_id=1, source_target_pairs={{0,16},{4,20},{8,24},{12,28},{16,0},{20,4},{24,8},{28,12},{1,17},{... | collective-permute-start | bytes 1382408 | tf_op jit(solution)/shard_map/ppermute | solution.py:124
  28.2 98.1 %collective-permute-start.4 = (f32[225,512]{1,0:T(8,128)}, f32[225,512]{1,0:T(8,128)S(1)}, u32[]{:S(2)}, u32[]{:S(2)}) collective-permute-start(f32[225,512]{1,0:T(8,128)} %get-tuple-element.210), channel_id=1, source_target_pairs={{0,12},{4,8},{8,4},{12,0},{16,28},{20,24},{24,20},{28,16},{1,13},{... | collective-permute-start | bytes 1382408 | tf_op jit(solution)/shard_map/ppermute | solution.py:124
  37.5 88.9 %collective-permute-start.5 = (f32[225,512]{1,0:T(8,128)}, f32[225,512]{1,0:T(8,128)S(1)}, u32[]{:S(2)}, u32[]{:S(2)}) collective-permute-start(f32[225,512]{1,0:T(8,128)} %get-tuple-element.211), channel_id=1, source_target_pairs={{0,8},{4,12},{8,0},{12,4},{16,24},{20,28},{24,16},{28,20},{1,9},{5... | collective-permute-start | bytes 1382408 | tf_op jit(solution)/shard_map/ppermute | solution.py:124
  96.5 51.3 %collective-permute-start.6 = (f32[225,512]{1,0:T(8,128)}, f32[225,512]{1,0:T(8,128)S(1)}, u32[]{:S(2)}, u32[]{:S(2)}) collective-permute-start(f32[225,512]{1,0:T(8,128)} %get-tuple-element.212), channel_id=1, source_target_pairs={{0,4},{4,0},{8,12},{12,8},{16,20},{20,16},{24,28},{28,24},{1,5},{5... | collective-permute-start | bytes 1382408 | tf_op jit(solution)/shard_map/ppermute | solution.py:124
  103.7 46.6 %collective-permute-start.7 = (f32[225,512]{1,0:T(8,128)}, f32[225,512]{1,0:T(8,128)S(1)}, u32[]{:S(2)}, u32[]{:S(2)}) collective-permute-start(f32[225,512]{1,0:T(8,128)} %get-tuple-element.240), channel_id=1, source_target_pairs={{0,28},{4,24},{8,20},{12,16},{16,12},{20,8},{24,4},{28,0},{1,29},{... | collective-permute-start | bytes 1382408 | tf_op jit(solution)/shard_map/ppermute | solution.py:124
  123.9 28.8 %collective-permute-start.8 = (f32[225,512]{1,0:T(8,128)}, f32[225,512]{1,0:T(8,128)S(1)}, u32[]{:S(2)}, u32[]{:S(2)}) collective-permute-start(f32[225,512]{1,0:T(8,128)} %get-tuple-element.241), channel_id=1, source_target_pairs={{0,24},{4,28},{8,16},{12,20},{16,8},{20,12},{24,0},{28,4},{1,25},{... | collective-permute-start | bytes 1382408 | tf_op jit(solution)/shard_map/ppermute | solution.py:124
  126.3 99.6 %collective-permute-start.9 = (f32[225,512]{1,0:T(8,128)}, f32[225,512]{1,0:T(8,128)S(1)}, u32[]{:S(2)}, u32[]{:S(2)}) collective-permute-start(f32[225,512]{1,0:T(8,128)} %get-tuple-element.242), channel_id=1, source_target_pairs={{0,20},{4,16},{8,28},{12,24},{16,4},{20,0},{24,12},{28,8},{1,21},{... | collective-permute-start | bytes 1382408 | tf_op jit(solution)/shard_map/ppermute | solution.py:124
  126.4 109.5 %collective-permute-start.10 = (f32[225,512]{1,0:T(8,128)}, f32[225,512]{1,0:T(8,128)S(1)}, u32[]{:S(2)}, u32[]{:S(2)}) collective-permute-start(f32[225,512]{1,0:T(8,128)} %get-tuple-element.243), channel_id=1, source_target_pairs={{0,16},{4,20},{8,24},{12,28},{16,0},{20,4},{24,8},{28,12},{1,17},{... | collective-permute-start | bytes 1382408 | tf_op jit(solution)/shard_map/ppermute | solution.py:124
  147.9 131.7 %collective-permute-start.14 = (f32[225,1024]{1,0:T(8,128)}, f32[225,1024]{1,0:T(8,128)}, u32[]{:S(2)}, u32[]{:S(2)}) collective-permute-start(f32[225,1024]{1,0:T(8,128)} %get-tuple-element.275), channel_id=1, source_target_pairs={{0,28},{4,24},{8,20},{12,16},{16,12},{20,8},{24,4},{28,0},{1,29},{... | collective-permute-start | bytes 2764808 | tf_op jit(solution)/shard_map/ppermute | solution.py:124
  150.3 184.6 %copy-start.6 = (f32[225,512]{1,0:T(8,128)}, f32[225,512]{1,0:T(8,128)S(1)}, u32[]{:S(2)}) copy-start(f32[225,512]{1,0:T(8,128)S(1)} %collective-permute-done.7.refs_1_) | copy-start | bytes 1382404
  150.3 152.1 %collective-permute-start.15 = (f32[225,1024]{1,0:T(8,128)}, f32[225,1024]{1,0:T(8,128)}, u32[]{:S(2)}, u32[]{:S(2)}) collective-permute-start(f32[225,1024]{1,0:T(8,128)} %get-tuple-element.276), channel_id=1, source_target_pairs={{0,24},{4,28},{8,16},{12,20},{16,8},{20,12},{24,0},{28,4},{1,25},{... | collective-permute-start | bytes 2764808 | tf_op jit(solution)/shard_map/ppermute | solution.py:124
  152.7 92.7 %collective-permute-start.11 = (f32[225,512]{1,0:T(8,128)}, f32[225,512]{1,0:T(8,128)S(1)}, u32[]{:S(2)}, u32[]{:S(2)}) collective-permute-start(f32[225,512]{1,0:T(8,128)} %get-tuple-element.244), channel_id=1, source_target_pairs={{0,12},{4,8},{8,4},{12,0},{16,28},{20,24},{24,20},{28,16},{1,13},{... | collective-permute-start | bytes 1382408 | tf_op jit(solution)/shard_map/ppermute | solution.py:124
  225.9 29.5 %collective-permute-start.12 = (f32[225,512]{1,0:T(8,128)}, f32[225,512]{1,0:T(8,128)S(1)}, u32[]{:S(2)}, u32[]{:S(2)}) collective-permute-start(f32[225,512]{1,0:T(8,128)} %get-tuple-element.245), channel_id=1, source_target_pairs={{0,8},{4,12},{8,0},{12,4},{16,24},{20,28},{24,16},{28,20},{1,9},{5... | collective-permute-start | bytes 1382408 | tf_op jit(solution)/shard_map/ppermute | solution.py:124
  236.0 20.2 %collective-permute-start.13 = (f32[225,512]{1,0:T(8,128)}, f32[225,512]{1,0:T(8,128)}, u32[]{:S(2)}, u32[]{:S(2)}) collective-permute-start(f32[225,512]{1,0:T(8,128)} %get-tuple-element.246), channel_id=1, source_target_pairs={{0,4},{4,0},{8,12},{12,8},{16,20},{20,16},{24,28},{28,24},{1,5},{5... | collective-permute-start | bytes 1382408 | tf_op jit(solution)/shard_map/ppermute | solution.py:124
  245.4 96.2 %collective-permute-start.16 = (f32[225,1024]{1,0:T(8,128)}, f32[225,1024]{1,0:T(8,128)S(1)}, u32[]{:S(2)}, u32[]{:S(2)}) collective-permute-start(f32[225,1024]{1,0:T(8,128)} %get-tuple-element.277), channel_id=1, source_target_pairs={{0,20},{4,16},{8,28},{12,24},{16,4},{20,0},{24,12},{28,8},{1,21},{... | collective-permute-start | bytes 2764808 | tf_op jit(solution)/shard_map/ppermute | solution.py:124
  255.5 117.5 %collective-permute-start.17 = (f32[225,1024]{1,0:T(8,128)}, f32[225,1024]{1,0:T(8,128)S(1)}, u32[]{:S(2)}, u32[]{:S(2)}) collective-permute-start(f32[225,1024]{1,0:T(8,128)} %get-tuple-element.278), channel_id=1, source_target_pairs={{0,16},{4,20},{8,24},{12,28},{16,0},{20,4},{24,8},{28,12},{1,17},{... | collective-permute-start | bytes 2764808 | tf_op jit(solution)/shard_map/ppermute | solution.py:124
  256.2 119.1 %collective-permute-start.18 = (f32[225,1024]{1,0:T(8,128)}, f32[225,1024]{1,0:T(8,128)S(1)}, u32[]{:S(2)}, u32[]{:S(2)}) collective-permute-start(f32[225,1024]{1,0:T(8,128)} %get-tuple-element.279), channel_id=1, source_target_pairs={{0,12},{4,8},{8,4},{12,0},{16,28},{20,24},{24,20},{28,16},{1,13},{... | collective-permute-start | bytes 2764808 | tf_op jit(solution)/shard_map/ppermute | solution.py:124
  279.5 95.8 %collective-permute-start.19 = (f32[225,1024]{1,0:T(8,128)}, f32[225,1024]{1,0:T(8,128)}, u32[]{:S(2)}, u32[]{:S(2)}) collective-permute-start(f32[225,1024]{1,0:T(8,128)} %get-tuple-element.280), channel_id=1, source_target_pairs={{0,8},{4,12},{8,0},{12,4},{16,24},{20,28},{24,16},{28,20},{1,9},{5... | collective-permute-start | bytes 2764808 | tf_op jit(solution)/shard_map/ppermute | solution.py:124
  302.4 74.9 %collective-permute-start.20 = (f32[225,1024]{1,0:T(8,128)}, f32[225,1024]{1,0:T(8,128)}, u32[]{:S(2)}, u32[]{:S(2)}) collective-permute-start(f32[225,1024]{1,0:T(8,128)} %get-tuple-element.281), channel_id=1, source_target_pairs={{0,4},{4,0},{8,12},{12,8},{16,20},{20,16},{24,28},{28,24},{1,5},{5... | collective-permute-start | bytes 2764808 | tf_op jit(solution)/shard_map/ppermute | solution.py:124
  341.6 39.1 %collective-permute-start.28 = (f32[225,512]{1,0:T(8,128)}, f32[225,512]{1,0:T(8,128)S(1)}, u32[]{:S(2)}, u32[]{:S(2)}) collective-permute-start(f32[225,512]{1,0:T(8,128)} %get-tuple-element.303), channel_id=1, source_target_pairs={{0,28},{4,24},{8,20},{12,16},{16,12},{20,8},{24,4},{28,0},{1,29},{... | collective-permute-start | bytes 1382408 | tf_op jit(solution)/shard_map/ppermute | solution.py:124
  373.0 15.8 %collective-permute-start.29 = (f32[225,512]{1,0:T(8,128)}, f32[225,512]{1,0:T(8,128)S(1)}, u32[]{:S(2)}, u32[]{:S(2)}) collective-permute-start(f32[225,512]{1,0:T(8,128)} %get-tuple-element.304), channel_id=1, source_target_pairs={{0,24},{4,28},{8,16},{12,20},{16,8},{20,12},{24,0},{28,4},{1,25},{... | collective-permute-start | bytes 1382408 | tf_op jit(solution)/shard_map/ppermute | solution.py:124
  375.4 109.7 %copy-start.5 = (f32[225,1024]{1,0:T(8,128)}, f32[225,1024]{1,0:T(8,128)S(1)}, u32[]{:S(2)}) copy-start(f32[225,1024]{1,0:T(8,128)S(1)} %collective-permute-done.18.refs_5_) | copy-start | bytes 2764804
  375.4 98.6 %collective-permute-start.30 = (f32[225,512]{1,0:T(8,128)}, f32[225,512]{1,0:T(8,128)S(1)}, u32[]{:S(2)}, u32[]{:S(2)}) collective-permute-start(f32[225,512]{1,0:T(8,128)} %get-tuple-element.305), channel_id=1, source_target_pairs={{0,20},{4,16},{8,28},{12,24},{16,4},{20,0},{24,12},{28,8},{1,21},{... | collective-permute-start | bytes 1382408 | tf_op jit(solution)/shard_map/ppermute | solution.py:124
  375.4 109.7 %collective-permute-start.31 = (f32[225,512]{1,0:T(8,128)}, f32[225,512]{1,0:T(8,128)S(1)}, u32[]{:S(2)}, u32[]{:S(2)}) collective-permute-start(f32[225,512]{1,0:T(8,128)} %get-tuple-element.306), channel_id=1, source_target_pairs={{0,16},{4,20},{8,24},{12,28},{16,0},{20,4},{24,8},{28,12},{1,17},{... | collective-permute-start | bytes 1382408 | tf_op jit(solution)/shard_map/ppermute | solution.py:124
  377.3 150.9 %collective-permute-start.21 = (f32[225,1024]{1,0:T(8,128)}, f32[225,1024]{1,0:T(8,128)S(1)}, u32[]{:S(2)}, u32[]{:S(2)}) collective-permute-start(f32[225,1024]{1,0:T(8,128)} %get-tuple-element.294), channel_id=1, source_target_pairs={{0,28},{4,24},{8,20},{12,16},{16,12},{20,8},{24,4},{28,0},{1,29},{... | collective-permute-start | bytes 2764808 | tf_op jit(solution)/shard_map/ppermute | solution.py:124
  380.7 304.0 %copy-start.12 = (f32[225,512]{1,0:T(8,128)}, f32[225,512]{1,0:T(8,128)S(1)}, u32[]{:S(2)}) copy-start(f32[225,512]{1,0:T(8,128)S(1)} %collective-permute-done.28.refs_1_) | copy-start | bytes 1382404
  380.7 170.6 %collective-permute-start.22 = (f32[225,1024]{1,0:T(8,128)}, f32[225,1024]{1,0:T(8,128)S(1)}, u32[]{:S(2)}, u32[]{:S(2)}) collective-permute-start(f32[225,1024]{1,0:T(8,128)} %get-tuple-element.295), channel_id=1, source_target_pairs={{0,24},{4,28},{8,16},{12,20},{16,8},{20,12},{24,0},{28,4},{1,25},{... | collective-permute-start | bytes 2764808 | tf_op jit(solution)/shard_map/ppermute | solution.py:124
  388.8 162.5 %copy-start.13 = (f32[225,512]{1,0:T(8,128)}, f32[225,512]{1,0:T(8,128)S(1)}, u32[]{:S(2)}) copy-start(f32[225,512]{1,0:T(8,128)S(1)} %collective-permute-done.29.refs_2_) | copy-start | bytes 1382404
  388.8 104.6 %collective-permute-start.32 = (f32[225,512]{1,0:T(8,128)}, f32[225,512]{1,0:T(8,128)S(1)}, u32[]{:S(2)}, u32[]{:S(2)}) collective-permute-start(f32[225,512]{1,0:T(8,128)} %get-tuple-element.307), channel_id=1, source_target_pairs={{0,12},{4,8},{8,4},{12,0},{16,28},{20,24},{24,20},{28,16},{1,13},{... | collective-permute-start | bytes 1382408 | tf_op jit(solution)/shard_map/ppermute | solution.py:124
  474.0 30.5 %collective-permute-start.33 = (f32[225,512]{1,0:T(8,128)}, f32[225,512]{1,0:T(8,128)S(1)}, u32[]{:S(2)}, u32[]{:S(2)}) collective-permute-start(f32[225,512]{1,0:T(8,128)} %get-tuple-element.308), channel_id=1, source_target_pairs={{0,8},{4,12},{8,0},{12,4},{16,24},{20,28},{24,16},{28,20},{1,9},{5... | collective-permute-start | bytes 1382408 | tf_op jit(solution)/shard_map/ppermute | solution.py:124
  485.0 19.5 %collective-permute-start.34 = (f32[225,512]{1,0:T(8,128)}, f32[225,512]{1,0:T(8,128)S(1)}, u32[]{:S(2)}, u32[]{:S(2)}) collective-permute-start(f32[225,512]{1,0:T(8,128)} %get-tuple-element.309), channel_id=1, source_target_pairs={{0,4},{4,0},{8,12},{12,8},{16,20},{20,16},{24,28},{28,24},{1,5},{5... | collective-permute-start | bytes 1382408 | tf_op jit(solution)/shard_map/ppermute | solution.py:124
  493.4 95.2 %collective-permute-start.23 = (f32[225,1024]{1,0:T(8,128)}, f32[225,1024]{1,0:T(8,128)S(1)}, u32[]{:S(2)}, u32[]{:S(2)}) collective-permute-start(f32[225,1024]{1,0:T(8,128)} %get-tuple-element.296), channel_id=1, source_target_pairs={{0,20},{4,16},{8,28},{12,24},{16,4},{20,0},{24,12},{28,8},{1,21},{... | collective-permute-start | bytes 2764808 | tf_op jit(solution)/shard_map/ppermute | solution.py:124
  504.5 118.6 %collective-permute-start.24 = (f32[225,1024]{1,0:T(8,128)}, f32[225,1024]{1,0:T(8,128)}, u32[]{:S(2)}, u32[]{:S(2)}) collective-permute-start(f32[225,1024]{1,0:T(8,128)} %get-tuple-element.297), channel_id=1, source_target_pairs={{0,16},{4,20},{8,24},{12,28},{16,0},{20,4},{24,8},{28,12},{1,17},{... | collective-permute-start | bytes 2764808 | tf_op jit(solution)/shard_map/ppermute | solution.py:124
  504.6 120.8 %collective-permute-start.25 = (f32[225,1024]{1,0:T(8,128)}, f32[225,1024]{1,0:T(8,128)}, u32[]{:S(2)}, u32[]{:S(2)}) collective-permute-start(f32[225,1024]{1,0:T(8,128)} %get-tuple-element.298), channel_id=1, source_target_pairs={{0,12},{4,8},{8,4},{12,0},{16,28},{20,24},{24,20},{28,16},{1,13},{... | collective-permute-start | bytes 2764808 | tf_op jit(solution)/shard_map/ppermute | solution.py:124
  528.3 156.4 %copy-start = (f32[225,1024]{1,0:T(8,128)}, f32[225,1024]{1,0:T(8,128)S(1)}, u32[]{:S(2)}) copy-start(f32[225,1024]{1,0:T(8,128)S(1)} %collective-permute-done.21.refs_1_) | copy-start | bytes 2764804
  528.3 97.1 %collective-permute-start.26 = (f32[225,1024]{1,0:T(8,128)}, f32[225,1024]{1,0:T(8,128)}, u32[]{:S(2)}, u32[]{:S(2)}) collective-permute-start(f32[225,1024]{1,0:T(8,128)} %get-tuple-element.299), channel_id=1, source_target_pairs={{0,8},{4,12},{8,0},{12,4},{16,24},{20,28},{24,16},{28,20},{1,9},{5... | collective-permute-start | bytes 2764808 | tf_op jit(solution)/shard_map/ppermute | solution.py:124
  551.4 133.3 %copy-start.1 = (f32[225,1024]{1,0:T(8,128)}, f32[225,1024]{1,0:T(8,128)S(1)}, u32[]{:S(2)}) copy-start(f32[225,1024]{1,0:T(8,128)S(1)} %collective-permute-done.22.refs_2_) | copy-start | bytes 2764804
  551.4 74.1 %collective-permute-start.27 = (f32[225,1024]{1,0:T(8,128)}, f32[225,1024]{1,0:T(8,128)}, u32[]{:S(2)}, u32[]{:S(2)}) collective-permute-start(f32[225,1024]{1,0:T(8,128)} %get-tuple-element.300), channel_id=1, source_target_pairs={{0,4},{4,0},{8,12},{12,8},{16,20},{20,16},{24,28},{28,24},{1,5},{5... | collective-permute-start | bytes 2764808 | tf_op jit(solution)/shard_map/ppermute | solution.py:124
  588.6 50.8 %collective-permute-start.35 = (f32[225,512]{1,0:T(8,128)}, f32[225,512]{1,0:T(8,128)}, u32[]{:S(2)}, u32[]{:S(2)}) collective-permute-start(f32[225,512]{1,0:T(8,128)} %get-tuple-element.313), channel_id=1, source_target_pairs={{0,28},{4,24},{8,20},{12,16},{16,12},{20,8},{24,4},{28,0},{1,29},{... | collective-permute-start | bytes 1382408 | tf_op jit(solution)/shard_map/ppermute | solution.py:124
  623.1 41.9 %collective-permute-start.36 = (f32[225,512]{1,0:T(8,128)}, f32[225,512]{1,0:T(8,128)}, u32[]{:S(2)}, u32[]{:S(2)}) collective-permute-start(f32[225,512]{1,0:T(8,128)} %get-tuple-element.314), channel_id=1, source_target_pairs={{0,24},{4,28},{8,16},{12,20},{16,8},{20,12},{24,0},{28,4},{1,25},{... | collective-permute-start | bytes 1382408 | tf_op jit(solution)/shard_map/ppermute | solution.py:124
  625.4 127.8 %collective-permute-start.37 = (f32[225,512]{1,0:T(8,128)}, f32[225,512]{1,0:T(8,128)}, u32[]{:S(2)}, u32[]{:S(2)}) collective-permute-start(f32[225,512]{1,0:T(8,128)} %get-tuple-element.315), channel_id=1, source_target_pairs={{0,20},{4,16},{8,28},{12,24},{16,4},{20,0},{24,12},{28,8},{1,21},{... | collective-permute-start | bytes 1382408 | tf_op jit(solution)/shard_map/ppermute | solution.py:124
  625.4 127.8 %collective-permute-start.38 = (f32[225,512]{1,0:T(8,128)}, f32[225,512]{1,0:T(8,128)}, u32[]{:S(2)}, u32[]{:S(2)}) collective-permute-start(f32[225,512]{1,0:T(8,128)} %get-tuple-element.316), channel_id=1, source_target_pairs={{0,16},{4,20},{8,24},{12,28},{16,0},{20,4},{24,8},{28,12},{1,17},{... | collective-permute-start | bytes 1382408 | tf_op jit(solution)/shard_map/ppermute | solution.py:124
  625.5 127.7 %collective-permute-start.39 = (f32[225,512]{1,0:T(8,128)}, f32[225,512]{1,0:T(8,128)}, u32[]{:S(2)}, u32[]{:S(2)}) collective-permute-start(f32[225,512]{1,0:T(8,128)} %get-tuple-element.317), channel_id=1, source_target_pairs={{0,12},{4,8},{8,4},{12,0},{16,28},{20,24},{24,20},{28,16},{1,13},{... | collective-permute-start | bytes 1382408 | tf_op jit(solution)/shard_map/ppermute | solution.py:124
  639.4 113.7 %collective-permute-start.40 = (f32[225,512]{1,0:T(8,128)}, f32[225,512]{1,0:T(8,128)}, u32[]{:S(2)}, u32[]{:S(2)}) collective-permute-start(f32[225,512]{1,0:T(8,128)} %get-tuple-element.318), channel_id=1, source_target_pairs={{0,8},{4,12},{8,0},{12,4},{16,24},{20,28},{24,16},{28,20},{1,9},{5... | collective-permute-start | bytes 1382408 | tf_op jit(solution)/shard_map/ppermute | solution.py:124
  664.9 88.3 %collective-permute-start.41 = (f32[225,512]{1,0:T(8,128)}, f32[225,512]{1,0:T(8,128)}, u32[]{:S(2)}, u32[]{:S(2)}) collective-permute-start(f32[225,512]{1,0:T(8,128)} %get-tuple-element.319), channel_id=1, source_target_pairs={{0,4},{4,0},{8,12},{12,8},{16,20},{20,16},{24,28},{28,24},{1,5},{5... | collective-permute-start | bytes 1382408 | tf_op jit(solution)/shard_map/ppermute | solution.py:124
  (19 other events, 799.9 us)
